TPU v7x, 128 devices: a whole 4x4x4 slice. The times are simulated.
128 devices in a mesh: ctx: 32 (over y, z, core), head: 4 (over x).
Axes of the slice: x: 4, y: 4, z: 4, core: 2. Of those that a mesh axis runs over, the one named last changes fastest.
Arguments:
- query: bfloat16 [65536, 2048], P('ctx', 'head'), may hold values from -6 to 6
- key: bfloat16 [65536, 2048], P('ctx', 'head'), may hold values from -6 to 6
- value: bfloat16 [65536, 2048], P('ctx', 'head'), may hold values from -6 to 6
- gain: bfloat16 [2048], P('head'), may hold values from 0.099609375 to 1.8984375
- w_out: bfloat16 [2048, 2048], replicated, may hold values from -0.125 to 0.125
- d_out: bfloat16 [65536, 2048], P(('ctx', 'head')), may hold values from -6 to 6
Outputs:
- out: bfloat16 [65536, 2048], P(('ctx', 'head'))
- grad_query: bfloat16 [65536, 2048], P('ctx', 'head')
- grad_key: bfloat16 [65536, 2048], P('ctx', 'head')
- grad_value: bfloat16 [65536, 2048], P('ctx', 'head')
All inputs are finite; a program needn't handle non-finite values.
Results may differ from a plain program's by a relative error of at most 0.018.
Values may be sent and summed in bfloat16 or wider, within the bound.
A program may use at most 128 MiB of HBM per device.

v0:
```python
import jax
import jax.numpy as jnp
from jax import lax
from jax.sharding import Mesh
from jax.sharding import PartitionSpec as P

HDIM = 128
BLOCK = 128
CTX = ("ctx_0", "ctx_1", "ctx_2")
CTX_HEAD = ("ctx_0", "ctx_1", "ctx_2", "head")


epsilon = 1e-06


def nothing_yet(value, identity):
    return jnp.broadcast_to(jnp.asarray(identity, value.dtype), value.shape)


def prefix_by_axis(value, axes, combine, identity, reverse):
    before = start = nothing_yet(value, identity)
    total = value
    for axis in reversed(axes):
        length, mine = (lax.axis_size(axis), lax.axis_index(axis))
        pieces = lax.all_gather(total.astype(jnp.bfloat16), axis)
        inside, total = (start, start)
        for k in reversed(range(length)) if reverse else range(length):
            passed = k > mine if reverse else k < mine
            total = combine(total, pieces[k].astype(value.dtype))
            inside = jnp.where(passed, total, inside)
        before = combine(inside, before)
    return before


def add_states(earlier, later):
    return earlier + later


def earlier_states(local_total):
    return prefix_by_axis(local_total, CTX, add_states, jnp.zeros_like(local_total), False)


def later_states(local_total):
    return prefix_by_axis(local_total, CTX, add_states, jnp.zeros_like(local_total), True)


def on_device(query, key, value, gain, w_out, d_out):
    tokens, width = query.shape
    local_heads = width // HDIM
    nblocks = tokens // BLOCK
    causal = jnp.tril(jnp.ones((BLOCK, BLOCK), dtype=bool))[None, None]

    def split_blocks(array):
        return array.reshape(nblocks, BLOCK, local_heads, HDIM)

    def masked(scores):
        return jnp.where(causal, scores, jnp.zeros_like(scores)).astype(jnp.bfloat16)

    q_blocks = split_blocks(query)
    k_blocks = split_blocks(key)
    v_blocks = split_blocks(value)
    scores = masked(
        jnp.einsum("cshe,cthe->chst", q_blocks, k_blocks, preferred_element_type=jnp.float32)
    )
    block_states = jnp.einsum(
        "cshe,cshf->chef", k_blocks, v_blocks, preferred_element_type=jnp.float32
    )
    before = earlier_states(jnp.sum(block_states, axis=0))
    running = jnp.cumsum(block_states, axis=0)
    inner_before = jnp.concatenate([jnp.zeros_like(running[:1]), running[:-1]], axis=0)
    prefixes = (before[None] + inner_before).astype(jnp.bfloat16)
    attended = jnp.einsum("chst,cthf->cshf", scores, v_blocks, preferred_element_type=jnp.float32)
    attended = attended + jnp.einsum(
        "cshe,chef->cshf", q_blocks, prefixes, preferred_element_type=jnp.float32
    )
    attended = attended.reshape(tokens, local_heads, HDIM)
    inverse = lax.rsqrt(jnp.mean(attended * attended, axis=-1, keepdims=True) + epsilon)
    unit = attended * inverse
    scales = gain.astype(jnp.float32).reshape(local_heads, HDIM)
    normed = (unit * scales).astype(jnp.bfloat16).reshape(tokens, width)
    w_slice = lax.dynamic_slice_in_dim(w_out, lax.axis_index("head") * width, width, 0)
    out = lax.psum_scatter(
        jnp.dot(normed, w_slice, preferred_element_type=jnp.float32).astype(jnp.bfloat16),
        "head",
        scatter_dimension=0,
        tiled=True,
    )
    grad_heads = lax.dot_general(
        lax.all_gather(d_out, "head", axis=0, tiled=True),
        w_slice,
        (((1,), (1,)), ((), ())),
        preferred_element_type=jnp.float32,
    ).astype(jnp.bfloat16)
    grad_unit = grad_heads.astype(jnp.float32).reshape(tokens, local_heads, HDIM) * scales
    grad_attended = inverse * (
        grad_unit - unit * jnp.mean(grad_unit * unit, axis=-1, keepdims=True)
    )
    g_blocks = split_blocks(grad_attended.astype(jnp.bfloat16))
    grad_scores = masked(
        jnp.einsum("cshf,cthf->chst", g_blocks, v_blocks, preferred_element_type=jnp.float32)
    )
    block_grads = jnp.einsum(
        "cshe,cshf->chef", q_blocks, g_blocks, preferred_element_type=jnp.float32
    )
    after = later_states(jnp.sum(block_grads, axis=0))
    tail_sums = jnp.cumsum(block_grads[::-1], axis=0)[::-1]
    inner_after = jnp.concatenate([tail_sums[1:], jnp.zeros_like(tail_sums[:1])], axis=0)
    suffixes = (after[None] + inner_after).astype(jnp.bfloat16)
    grad_query = jnp.einsum(
        "chst,cthe->cshe", grad_scores, k_blocks, preferred_element_type=jnp.float32
    )
    grad_query = grad_query + jnp.einsum(
        "cshf,chef->cshe", g_blocks, prefixes, preferred_element_type=jnp.float32
    )
    grad_key = jnp.einsum(
        "chst,cshe->cthe", grad_scores, q_blocks, preferred_element_type=jnp.float32
    )
    grad_key = grad_key + jnp.einsum(
        "cthf,chef->cthe", v_blocks, suffixes, preferred_element_type=jnp.float32
    )
    grad_value = jnp.einsum("chst,cshf->cthf", scores, g_blocks, preferred_element_type=jnp.float32)
    grad_value = grad_value + jnp.einsum(
        "cthe,chef->cthf", k_blocks, suffixes, preferred_element_type=jnp.float32
    )
    return (
        out,
        grad_query.reshape(tokens, width).astype(jnp.bfloat16),
        grad_key.reshape(tokens, width).astype(jnp.bfloat16),
        grad_value.reshape(tokens, width).astype(jnp.bfloat16),
    )


def solution(mesh):
    finer = Mesh(
        mesh.devices.reshape(4, 4, 2, mesh.shape["head"]), ("ctx_0", "ctx_1", "ctx_2", "head")
    )
    in_specs = (P(CTX, "head"), P(CTX, "head"), P(CTX, "head"), P("head"), P(), P(CTX_HEAD, None))
    out_specs = (P(CTX_HEAD, None), P(CTX, "head"), P(CTX, "head"), P(CTX, "head"))
    return jax.shard_map(
        on_device, mesh=finer, in_specs=in_specs, out_specs=out_specs, check_vma=False
    )
```

profile of v0, /device:TPU:1, one launch (start us, length us, event | category | flops | bytes accessed | tf_op | source)
XLA Modules:
  0.0 211.9 jit_solution(12444934481127085550)
XLA Ops:
  8.0 2.6 %reshape.94 = bf16[16,128,4,128]{3,2,1,0:T(4,128)(2,1)S(1)} reshape(bf16[2048,512]{1,0:T(8,128)(2,1)} %param.6) | data formatting | bytes 4194304 | tf_op jit(solution)/shard_map/reshape | solution.py:54
  10.5 4.0 %reshape.95 = bf16[16,128,4,128]{3,2,1,0:T(4,128)(2,1)} reshape(bf16[2048,512]{1,0:T(8,128)(2,1)} %param.7) | data formatting | bytes 4194304 | tf_op jit(solution)/shard_map/reshape | solution.py:54
  14.5 4.0 %reshape.96 = bf16[16,128,4,128]{3,2,1,0:T(4,128)(2,1)} reshape(bf16[2048,512]{1,0:T(8,128)(2,1)} %param.8) | data formatting | bytes 4194304 | tf_op jit(solution)/shard_map/reshape | solution.py:54
  18.4 3.1 %fusion.61 = (bf16[4,128,128]{2,1,0:T(8,128)(2,1)S(1)}, f32[16,4,128,128]{3,2,1,0:T(8,128)S(1)}) fusion(bf16[16,128,4,128]{3,2,1,0:T(4,128)(2,1)} %reshape.96, bf16[16,128,4,128]{3,2,1,0:T(4,128)(2,1)} %reshape.95), kind=kOutput, calls=%fused_computation.99 | convolution fusion | flops 269418496 | bytes 8519680 | tf_op jit(solution)/shard_map/cshe,cshf->chef/dot_general | solution.py:65
  21.6 6.4 %fusion.63 = f32[16,4,128,128]{3,2,1,0:T(8,128)S(1)} fusion(f32[16,4,128,128]{3,2,1,0:T(8,128)S(1)} %get-tuple-element.17), kind=kOutput, calls=%fused_computation.101 | output fusion | flops 15728640 | bytes 8388608 | tf_op jit(solution)/shard_map/jit(cumsum)/reduce_window_sum | solution.py:69
  28.5 3.1 %all-gather = bf16[8,128,128]{2,1,0:T(8,128)(2,1)S(1)} all-gather(bf16[4,128,128]{2,1,0:T(8,128)(2,1)S(1)} %get-tuple-element.16), channel_id=2, replica_groups=mesh['ctx_0'=4,'ctx_1'=4,'ctx_2'=2,'head'=4] {'ctx_2'}, dimensions={0}, use_global_device_ids=true | all-gather | bytes 393216 | tf_op jit(solution)/shard_map/all_gather | solution.py:25
  31.7 13.2 %all_gather.28 = bf16[4,4,128,128]{3,2,1,0:T(8,128)(2,1)S(1)} all-gather(bf16[1,4,128,128]{3,2,1,0:T(8,128)(2,1)S(1)} %fusion.52), channel_id=1, replica_groups=mesh['ctx_0'=4,'ctx_1'=4,'ctx_2'=2,'head'=4] {'ctx_1'}, dimensions={0}, use_global_device_ids=true | all-gather | bytes 655360 | tf_op jit(solution)/shard_map/all_gather | solution.py:25
  45.0 12.4 %all_gather.29 = bf16[4,4,128,128]{3,2,1,0:T(8,128)(2,1)S(1)} all-gather(bf16[1,4,128,128]{3,2,1,0:T(8,128)(2,1)S(1)} %fusion.51), channel_id=1, replica_groups=mesh['ctx_0'=4,'ctx_1'=4,'ctx_2'=2,'head'=4] {'ctx_0'}, dimensions={0}, use_global_device_ids=true | all-gather | bytes 655360 | tf_op jit(solution)/shard_map/all_gather | solution.py:25
  61.3 3.5 %multiply_reduce_fusion = (f32[16,128,4]{1,2,0:T(4,128)S(1)}, f32[16,128,4,128]{3,1,2,0:T(8,128)}) fusion(f32[15,4,128,128]{3,2,1,0:T(8,128)S(1)} %slice.106, f32[4,128,128]{2,1,0:T(8,128)S(1)} %fusion.31, bf16[16,128,4,128]{3,2,1,0:T(4,128)(2,1)S(1)} %reshape.94, f32[16,4,128,128]{3,2,1,0:T(8,128)S(1)} %fusion.14), kind=kOutput, calls=%fused_computation.16 | convolution fusion | flops 273670144 | bytes 14712832 | tf_op jit(solution)/shard_map/cshe,chef->cshf/dot_general | solution.py:73
  64.8 5.6 %copy.66 = f32[16,128,4,128]{1,0,3,2:T(8,128)} copy(f32[16,128,4,128]{3,1,2,0:T(8,128)} %get-tuple-element.19) | data formatting | bytes 8388608 | tf_op jit(solution)/shard_map/add | solution.py:73
  70.4 4.0 %fusion.1 = bf16[2048,512]{0,1:T(8,128)(2,1)S(1)} fusion(f32[64,8,16,128]{3,2,1,0:T(8,128)} %bitcast.93, f32[2048,4]{0,1:T(4,128)S(1)} %get-tuple-element.13, f32[512]{0:T(512)S(1)} %get-tuple-element.15), kind=kLoop, calls=%fused_computation.3 | loop fusion | flops 3145728 | bytes 6326272 | tf_op jit(solution)/shard_map/convert_element_type | solution.py:80
  74.4 8.4 %convolution_convert_fusion = bf16[2048,2048]{1,0:T(8,128)(2,1)} fusion(bf16[2048,512]{0,1:T(8,128)(2,1)S(1)} %fusion.1, bf16[2048,2048]{1,0:T(8,128)(2,1)} %param.10, s32[]{:T(128)S(6)} %select_n.175), kind=kOutput, calls=%fused_computation | convolution fusion | flops 4299161600 | bytes 12582916 | tf_op jit(solution)/shard_map/dot_general | solution.py:83
  82.9 4.7 %copy.70 = f32[16,128,4,128]{3,1,0,2:T(8,128)} copy(f32[16,128,4,128]{3,1,2,0:T(8,128)} %get-tuple-element.19) | data formatting | bytes 8388608 | tf_op jit(solution)/shard_map/add | solution.py:73
  87.5 8.2 %all-gather.4.cloned.1.call-done = bf16[2048,2048]{1,0:T(8,128)(2,1)} async-done(((bf16[512,2048]{1,0:T(8,128)(2,1)}), bf16[2048,2048]{1,0:T(8,128)(2,1)}) %all-gather.4.cloned.1.call-update) | async-done | bytes 8388624 | tf_op jit(solution)/shard_map/all_gather | solution.py:89
  95.7 7.6 %fusion.6 = f32[512,2048]{1,0:T(8,128)S(1)} fusion(bf16[2048,2048]{1,0:T(8,128)(2,1)} %all-gather.4.cloned.1.call-done, bf16[2048,2048]{1,0:T(8,128)(2,1)} %param.10, s32[]{:T(128)S(6)} %select_n.175), kind=kOutput, calls=%fused_computation.20 | convolution fusion | flops 4297064448 | bytes 14680068 | tf_op jit(solution)/shard_map/dot_general | solution.py:88
  103.4 3.2 %copy.106 = f32[64,8,16,128]{3,2,1,0:T(8,128)} copy(f32[64,8,16,128]{3,1,2,0:T(8,128)S(1)} %bitcast.94) | data formatting | bytes 8388608
  106.6 5.4 %copy.68 = f32[16,128,4,128]{3,1,2,0:T(8,128)} copy(f32[16,128,4,128]{1,0,3,2:T(8,128)} %bitcast.96) | data formatting | bytes 8388608 | tf_op jit(solution)/shard_map/reshape | solution.py:94
  112.0 5.3 %copy.69 = f32[2048,4,128]{2,0,1:T(8,128)} copy(f32[2048,4,128]{0,2,1:T(8,128)} %bitcast.95) | data formatting | bytes 8388608 | tf_op jit(solution)/shard_map/reshape | solution.py:94
  117.4 4.9 %fusion.5 = f32[2048,4]{0,1:T(4,128)S(1)} fusion(f32[16,128,4,128]{3,1,0,2:T(8,128)} %copy.70, f32[2048,4,128]{2,0,1:T(8,128)} %copy.69, f32[4,128]{1,0:T(4,128)S(1)} %get-tuple-element.14, f32[2048,4]{0,1:T(4,128)S(1)} %get-tuple-element.13), kind=kLoop, calls=%fused_computation.10 | loop fusion | flops 4186112 | bytes 8456192 | tf_op jit(solution)/shard_map/reduce_sum | solution.py:96
  123.5 2.7 %multiply_convert_fusion = bf16[16,128,4,128]{3,1,2,0:T(8,128)(2,1)S(1)} fusion(f32[16,128,4,128]{3,1,2,0:T(8,128)S(1)} %copy-done, f32[16,128,4,128]{3,1,2,0:T(8,128)S(1)} %copy-done.12, f32[16,128,4]{1,2,0:T(4,128)S(1)} %multiply_bitcast_fusion, f32[4,128]{1,0:T(4,128)S(1)} %get-tuple-element.14, f32[16,128,4]{1,2,0:T(4,128)S(1)} %get-tuple-element.12), kind=kLoop, calls=%fused_computation.15 | loop fusion | flops 6291456 | bytes 10553344 | tf_op jit(solution)/shard_map/convert_element_type | solution.py:98
  136.5 2.9 %fusion.62 = (bf16[4,128,128]{1,2,0:T(8,128)(2,1)S(1)}, f32[16,4,128,128]{2,3,1,0:T(8,128)}) fusion(bf16[16,128,4,128]{3,1,2,0:T(8,128)(2,1)S(1)} %multiply_convert_fusion, bf16[16,128,4,128]{3,2,1,0:T(4,128)(2,1)S(1)} %reshape.94), kind=kOutput, calls=%fused_computation.100 | convolution fusion | flops 269418496 | bytes 8519680 | tf_op jit(solution)/shard_map/cshe,cshf->chef/dot_general | solution.py:102
  139.6 4.9 %rev.4 = f32[16,4,128,128]{2,3,1,0:T(8,128)} reverse(f32[16,4,128,128]{2,3,1,0:T(8,128)} %get-tuple-element.21), dimensions={0} | reverse | bytes 8388608 | tf_op jit(solution)/shard_map/rev | solution.py:106
  144.4 5.4 %copy.81 = f32[16,4,128,128]{3,2,1,0:T(8,128)} copy(f32[16,4,128,128]{2,3,1,0:T(8,128)} %rev.4) | data formatting | bytes 8388608 | tf_op jit(solution)/shard_map/rev | solution.py:106
  149.8 2.7 %fusion.64 = f32[16,4,128,128]{3,2,1,0:T(8,128)S(1)} fusion(f32[16,4,128,128]{3,2,1,0:T(8,128)} %copy.81), kind=kOutput, calls=%fused_computation.102 | output fusion | flops 15728640 | bytes 8388608 | tf_op jit(solution)/shard_map/jit(cumsum)/reduce_window_sum | solution.py:106
  152.6 2.3 %slice.117 = f32[15,4,128,128]{3,2,1,0:T(8,128)} slice(f32[16,4,128,128]{3,2,1,0:T(8,128)S(1)} %fusion.64), slice={[0:15], [0:4], [0:128], [0:128]} | slice | bytes 7864320 | tf_op jit(solution)/shard_map/slice | solution.py:107
  154.9 4.5 %slice.91 = f32[15,4,128,128]{3,2,1,0:T(8,128)} reverse(f32[15,4,128,128]{3,2,1,0:T(8,128)} %slice.117), dimensions={0} | reverse | bytes 7864320 | tf_op jit(solution)/shard_map/slice | solution.py:107
  159.4 2.6 %all-gather.1 = bf16[8,128,128]{2,1,0:T(8,128)(2,1)S(1)} all-gather(bf16[4,128,128]{2,1,0:T(8,128)(2,1)S(1)} %copy.80), channel_id=3, replica_groups=mesh['ctx_0'=4,'ctx_1'=4,'ctx_2'=2,'head'=4] {'ctx_2'}, dimensions={0}, use_global_device_ids=true | all-gather | bytes 393216 | tf_op jit(solution)/shard_map/all_gather | solution.py:25
  162.0 11.6 %all_gather.32 = bf16[4,4,128,128]{3,2,1,0:T(8,128)(2,1)S(1)} all-gather(bf16[1,4,128,128]{3,2,1,0:T(8,128)(2,1)S(1)} %fusion.53), channel_id=1, replica_groups=mesh['ctx_0'=4,'ctx_1'=4,'ctx_2'=2,'head'=4] {'ctx_1'}, dimensions={0}, use_global_device_ids=true | all-gather | bytes 655360 | tf_op jit(solution)/shard_map/all_gather | solution.py:25
  173.6 11.4 %all_gather.33 = bf16[4,4,128,128]{3,2,1,0:T(8,128)(2,1)S(1)} all-gather(bf16[1,4,128,128]{3,2,1,0:T(8,128)(2,1)S(1)} %fusion.50), channel_id=1, replica_groups=mesh['ctx_0'=4,'ctx_1'=4,'ctx_2'=2,'head'=4] {'ctx_0'}, dimensions={0}, use_global_device_ids=true | all-gather | bytes 655360 | tf_op jit(solution)/shard_map/all_gather | solution.py:25
  193.5 2.9 %fusion.9 = bf16[16,128,4,128]{1,3,2,0:T(8,128)(2,1)} fusion(f32[16,4,128,128]{3,2,1,0:T(8,128)S(1)} %fusion.65, bf16[16,128,4,128]{3,2,1,0:T(4,128)(2,1)S(1)} %copy-done.6, f32[15,4,128,128]{3,2,1,0:T(8,128)S(1)} %copy-done.3, f32[4,128,128]{2,1,0:T(8,128)S(1)} %fusion.40), kind=kOutput, calls=%fused_computation.27 | convolution fusion | flops 272629760 | bytes 12582912 | tf_op jit(solution)/shard_map/cthe,chef->cthf/dot_general | solution.py:122
  196.5 4.3 %copy.100 = bf16[16,128,4,128]{3,2,1,0:T(4,128)(2,1)} copy(bf16[16,128,4,128]{1,3,2,0:T(8,128)(2,1)} %fusion.9) | data formatting | bytes 4194304
  200.7 4.3 %copy_bitcast_fusion = (bf16[2048,512]{1,0:T(8,128)(2,1)}, bf16[2048,512]{1,0:T(8,128)(2,1)}) fusion(bf16[256,8,4,128]{3,2,1,0:T(4,128)(2,1)} %bitcast.99, bf16[256,8,4,128]{3,2,1,0:T(4,128)(2,1)S(1)} %bitcast.98), kind=kLoop, calls=%fused_computation.22 | loop fusion | bytes 8388608
  (66 shorter events, 25.3 us)
Async XLA Ops:
  7.2 88.6 %all-gather.4.cloned.1.call-start = ((), (), s32[]{:S(2)}) async-start(), calls=%async_computation.2 | async-start | bytes 10485760 | tf_op jit(solution)/shard_map/all_gather | solution.py:89
  7.9 197.1 %reduce-scatter.2.cloned.1.call-start = ((), (), s32[]{:S(2)}) async-start(), calls=%async_computation.1 | async-start | bytes 10485760 | tf_op jit(solution)/shard_map/reduce_scatter | solution.py:82
  28.5 32.8 %copy-start.1 = (f32[15,4,128,128]{3,2,1,0:T(8,128)}, f32[15,4,128,128]{3,2,1,0:T(8,128)S(1)}, u32[]{:S(2)}) copy-start(f32[15,4,128,128]{3,2,1,0:T(8,128)S(1)} %slice.106) | copy-start | bytes 11796484
  28.5 29.2 %copy-start.4 = (bf16[16,128,4,128]{3,2,1,0:T(4,128)(2,1)S(1)}, bf16[16,128,4,128]{3,2,1,0:T(4,128)(2,1)}, u32[]{:S(2)}) copy-start(bf16[16,128,4,128]{3,2,1,0:T(4,128)(2,1)} %reshape.95) | copy-start | bytes 6291460
  57.7 2.9 %copy-start.7 = (bf16[16,128,4,128]{3,2,1,0:T(4,128)(2,1)S(1)}, bf16[16,128,4,128]{3,2,1,0:T(4,128)(2,1)}, u32[]{:S(2)}) copy-start(bf16[16,128,4,128]{3,2,1,0:T(4,128)(2,1)} %reshape.96) | copy-start | bytes 6291460
  59.3 1.3 copy-start.14
  64.8 5.7 %copy-start.18 = (bf16[512]{0:T(512)(128)(2,1)S(1)}, bf16[512]{0:T(512)(128)(2,1)}, u32[]{:S(2)}) copy-start(bf16[512]{0:T(512)(128)(2,1)} %param.9) | copy-start | bytes 3076
  103.4 3.2 %copy-start.13 = (f32[512,2048]{1,0:T(8,128)}, f32[512,2048]{1,0:T(8,128)S(1)}, u32[]{:S(2)}) copy-start(f32[512,2048]{1,0:T(8,128)S(1)} %fusion.6) | copy-start | bytes 12582916
  117.4 4.9 %copy-start = (f32[16,128,4,128]{3,1,2,0:T(8,128)S(1)}, f32[16,128,4,128]{3,1,2,0:T(8,128)}, u32[]{:S(2)}) copy-start(f32[16,128,4,128]{3,1,2,0:T(8,128)} %get-tuple-element.19) | copy-start | bytes 12582916
  117.4 6.1 %copy-start.12 = (f32[16,128,4,128]{3,1,2,0:T(8,128)S(1)}, f32[16,128,4,128]{3,1,2,0:T(8,128)}, u32[]{:S(2)}) copy-start(f32[16,128,4,128]{3,1,2,0:T(8,128)} %copy.68) | copy-start | bytes 12582916
  123.5 2.8 %copy-start.8 = (bf16[16,128,4,128]{3,2,1,0:T(4,128)(2,1)S(1)}, bf16[16,128,4,128]{3,2,1,0:T(4,128)(2,1)}, u32[]{:S(2)}) copy-start(bf16[16,128,4,128]{3,2,1,0:T(4,128)(2,1)} %reshape.96) | copy-start | bytes 6291460
  126.2 10.3 %copy-start.10 = (bf16[16,128,4,128]{3,1,2,0:T(8,128)(2,1)}, bf16[16,128,4,128]{3,1,2,0:T(8,128)(2,1)S(1)}, u32[]{:S(2)}) copy-start(bf16[16,128,4,128]{3,1,2,0:T(8,128)(2,1)S(1)} %multiply_convert_fusion) | copy-start | bytes 6291460
  126.2 2.9 %copy-start.5 = (bf16[16,128,4,128]{3,2,1,0:T(4,128)(2,1)S(1)}, bf16[16,128,4,128]{3,2,1,0:T(4,128)(2,1)}, u32[]{:S(2)}) copy-start(bf16[16,128,4,128]{3,2,1,0:T(4,128)(2,1)} %reshape.95) | copy-start | bytes 6291460
  127.8 1.3 copy-start.16
  129.2 2.2 %copy-start.2 = (f32[15,4,128,128]{3,2,1,0:T(8,128)S(1)}, f32[15,4,128,128]{3,2,1,0:T(8,128)}, u32[]{:S(2)}) copy-start(f32[15,4,128,128]{3,2,1,0:T(8,128)} %copy-done.1) | copy-start | bytes 11796484
  159.4 26.0 %copy-start.17 = (bf16[16,4,128,128]{3,2,1,0:T(8,128)(2,1)S(1)}, bf16[16,4,128,128]{3,2,1,0:T(8,128)(2,1)}, u32[]{:S(2)}) copy-start(bf16[16,4,128,128]{3,2,1,0:T(8,128)(2,1)} %copy-done.16) | copy-start | bytes 6291460
  185.4 2.1 copy-start.3
  185.4 2.8 %copy-start.9 = (bf16[16,128,4,128]{3,2,1,0:T(4,128)(2,1)S(1)}, bf16[16,128,4,128]{3,2,1,0:T(4,128)(2,1)}, u32[]{:S(2)}) copy-start(bf16[16,128,4,128]{3,2,1,0:T(4,128)(2,1)} %reshape.96) | copy-start | bytes 6291460
  189.7 1.8 copy-start.11
  189.7 2.2 %copy-start.15 = (bf16[16,4,128,128]{3,2,1,0:T(8,128)(2,1)S(1)}, bf16[16,4,128,128]{3,2,1,0:T(8,128)(2,1)}, u32[]{:S(2)}) copy-start(bf16[16,4,128,128]{3,2,1,0:T(8,128)(2,1)} %copy-done.14) | copy-start | bytes 6291460
  191.9 1.6 copy-start.6
Sparse Core Ops, SparseCore 0:
  9.6 86.0 all-gather.3
  98.8 81.5 reduce-scatter.1
where the time goes:
time: 216 us; the launch traced here: 212 us
  local copies, waits for them, and re-layouts  74.6 us (35%)
  blocking collectives  54.4 us (25%)
  matrix products  38 us (18%)
  other arithmetic  21.5 us (10%)
  between operations  14.4 us (7%)
  waiting for transfers between devices  8.91 us (4%)
    all_gather x6, blocking collectives, prefix_by_axis(): pieces = lax.all_gather(total.astype(jnp.bfloat16), axis)  54.4 us
    unnamed x44, local copies, waits for them, and re-layouts  25.4 us
    reshape x2, local copies, waits for them, and re-layouts, on_device(): grad_heads.astype(jnp.float32).reshape(tokens, local_heads, HDIM) * scales  10.8 us
    reshape x3, local copies, waits for them, and re-layouts, split_blocks(): return array.reshape(nblocks, BLOCK, local_heads, HDIM)  10.5 us
    add x2, local copies, waits for them, and re-layouts, on_device(): attended + jnp.einsum('cshe,chef->cshf', q_blocks, prefixes, preferred_el...  10.3 us
    rev x2, local copies, waits for them, and re-layouts, on_device(): tail_sums = jnp.cumsum(block_grads[::-1], axis=0)[::-1]  10.3 us
    dot_general x1, matrix products, on_device(): jnp.dot(normed, w_slice, preferred_element_type=jnp.float32)  8.42 us
    all_gather x1, waiting for transfers between devices, on_device(): lax.all_gather(d_out, 'head', axis=0, tiled=True)  8.22 us
  transfers between devices with their start and end apart: 2, of which 1 were waited for; matrix products, arithmetic and copies ran while one was open for 59% of the time, Pallas kernels for 0%

commit v1 on v0

v1 whole, which is shorter than its diff:
```python
import jax
import jax.numpy as jnp
from jax import lax
from jax.experimental import pallas as pl
from jax.experimental.pallas import tpu as pltpu
from jax.sharding import PartitionSpec as P

HDIM = 128
BLOCK = 128
EPSILON = 1e-06
MESH = pl.DeviceIdType.MESH
F32 = jnp.float32
BF16 = jnp.bfloat16


def rows_of(index, size):
    return pl.ds(pl.multiple_of(index * size, size), size)


def dot_nn(a, b):
    return jnp.dot(a, b, preferred_element_type=F32)


def dot_nt(a, b):
    return lax.dot_general(a, b, (((1,), (1,)), ((), ())), preferred_element_type=F32)


def dot_tn(a, b):
    return lax.dot_general(a, b, (((0,), (0,)), ((), ())), preferred_element_type=F32)


def kernel(
    query, key, value, gain, w_out, d_out,
    out, grad_query, grad_key, grad_value,
    q, k, v, w, d, gn_send, gn, nm, nr, sc, gsc, g, pb, st, bg, unit, inv, sq, sk, sv, so,
    tb, ra, ea, rs, rb, pc, rc,
    load_sem, w_sem, gn_ssem, gn_rsem, nm_ssem, nm_rsem,
    a_ssem, a_rsem, b_ssem, b_rsem, c_ssem, c_rsem, gq_sem, gk_sem, gv_sem, out_sem,
):
    ci = lax.axis_index("ctx")
    hi = lax.axis_index("head")
    y = ci // 8
    me = lax.rem(ci, 8)
    heads = 4
    nblocks = 16

    pltpu.make_async_copy(d_out, d, load_sem.at[0]).start()

    def w_load(i):
        h = lax.rem(hi + (1 + 2 * i - 3 * (i // 2)) * (1 - i // 3), 4)
        return pltpu.make_async_copy(
            w_out.at[rows_of(h, 512), :], w.at[rows_of(h, 512), :], w_sem.at[i]
        )

    for i in range(4):
        w_load(i).start()
    loads = (
        pltpu.make_async_copy(key, k, load_sem.at[1]),
        pltpu.make_async_copy(value, v, load_sem.at[2]),
        pltpu.make_async_copy(query, q, load_sem.at[3]),
    )
    for load in loads:
        load.start()

    def near(i):
        return {"ctx": y * 8 + lax.rem(me + i, 8)}

    def far(i):
        return {"ctx": lax.rem(y + i, 4) * 8 + me}

    def across(o):
        return {"head": lax.rem(hi + o, 4)}

    barrier = pltpu.get_barrier_semaphore()
    for peer in (
        [across(o) for o in (1, 2, 3)]
        + [near(i) for i in range(1, 8)]
        + [far(i) for i in range(1, 4)]
    ):
        pl.semaphore_signal(barrier, inc=1, device_id=peer, device_id_type=MESH)
    pl.semaphore_wait(barrier, 13)

    def offset(j):
        return 1 + 2 * j - 3 * (j // 2)

    def gn_copy(j, half):
        return pltpu.make_async_remote_copy(
            src_ref=gn_send.at[j, rows_of(half, 256), :],
            dst_ref=gn.at[rows_of(hi * 2 + half, 256), :],
            send_sem=gn_ssem.at[j, half],
            recv_sem=gn_rsem.at[j, half],
            device_id=across(offset(j)),
            device_id_type=MESH,
        )

    def gn_arrival(j, half):
        source = lax.rem(hi - offset(j) + 4, 4)
        return pltpu.make_async_remote_copy(
            src_ref=gn_send.at[j, rows_of(half, 256), :],
            dst_ref=gn.at[rows_of(source * 2 + half, 256), :],
            send_sem=gn_ssem.at[j, half],
            recv_sem=gn_rsem.at[j, half],
            device_id=across(offset(j)),
            device_id_type=MESH,
        )

    pltpu.make_async_copy(d_out, d, load_sem.at[0]).wait()

    def gn_step(i, carry):
        half, j = i // 3, lax.rem(i, 3)

        @pl.when(half == 0)
        def _():
            w_load(j).wait()

        h = lax.rem(hi + offset(j), 4)
        gn_send[j, rows_of(half, 256), :] = dot_nt(
            d[rows_of(half, 256), :], w[rows_of(h, 512), :]
        ).astype(BF16)
        gn_copy(j, half).start()
        return carry

    lax.fori_loop(0, 6, gn_step, 0)

    loads[0].wait()
    loads[1].wait()
    st[0] = jnp.zeros((heads, HDIM, HDIM), F32)

    def state_step(b, carry):
        rows = rows_of(b, BLOCK)
        for h in range(heads):
            cols = slice(h * HDIM, (h + 1) * HDIM)
            st[b + 1, h] = st[b, h] + dot_tn(k[rows, cols], v[rows, cols])
        return carry

    lax.fori_loop(0, nblocks, state_step, 0)

    def a_copy(way, i, slot):
        return pltpu.make_async_remote_copy(
            src_ref=tb.at[way, rows_of(lax.rem(me + i, 8), 64), :],
            dst_ref=ra.at[way, slot],
            send_sem=a_ssem.at[way, i - 1],
            recv_sem=a_rsem.at[way, i - 1],
            device_id=near(i),
            device_id_type=MESH,
        )

    def b_copy(way, i, slot):
        return pltpu.make_async_remote_copy(
            src_ref=rs.at[way],
            dst_ref=rb.at[way, slot],
            send_sem=b_ssem.at[way, i - 1],
            recv_sem=b_rsem.at[way, i - 1],
            device_id=far(i),
            device_id_type=MESH,
        )

    def c_copy(way, i, slot):
        return pltpu.make_async_remote_copy(
            src_ref=pc.at[way, lax.rem(me + i, 8)],
            dst_ref=rc.at[way, rows_of(slot, 64), :],
            send_sem=c_ssem.at[way, i - 1],
            recv_sem=c_rsem.at[way, i - 1],
            device_id=near(i),
            device_id_type=MESH,
        )

    def exchange_a(way, total):
        tb[way] = total.reshape(heads * HDIM, HDIM).astype(BF16)
        ra[way, me] = tb[way, rows_of(me, 64), :]
        for i in range(1, 8):
            a_copy(way, i, me).start()

    def exchange_b(way):
        for i in range(1, 8):
            a_copy(way, i, lax.rem(me - i + 8, 8)).wait()
        run = jnp.zeros((64, HDIM), F32)
        for s in reversed(range(8)) if way else range(8):
            ea[way, s] = run
            run = run + ra[way, s].astype(F32)
        rs[way] = run
        rb[way, y] = jnp.zeros((64, HDIM), F32)
        for i in range(1, 4):
            b_copy(way, i, y).start()

    def exchange_c(way):
        for i in range(1, 4):
            b_copy(way, i, lax.rem(y - i + 4, 4)).wait()
        base = jnp.zeros((64, HDIM), F32)
        for s in range(4):
            passed = s > y if way else s < y
            base = base + jnp.where(passed, rb[way, s], jnp.zeros((64, HDIM), F32))
        for s in range(8):
            pc[way, s] = (base + ea[way, s]).astype(BF16)
        rc[way, rows_of(me, 64), :] = pc[way, me]
        for i in range(1, 8):
            c_copy(way, i, me).start()

    def exchange_end(way):
        for i in range(1, 8):
            c_copy(way, i, lax.rem(me - i + 8, 8)).wait()

    exchange_a(0, st[nblocks])

    loads[2].wait()

    def causal(scores):
        row = lax.broadcasted_iota(jnp.int32, (BLOCK, BLOCK), 0)
        col = lax.broadcasted_iota(jnp.int32, (BLOCK, BLOCK), 1)
        return jnp.where(col <= row, scores, jnp.zeros_like(scores)).astype(BF16)

    def score_step(b, carry):
        rows = rows_of(b, BLOCK)
        for h in range(heads):
            cols = slice(h * HDIM, (h + 1) * HDIM)
            sc[b, h] = causal(dot_nt(q[rows, cols], k[rows, cols]))
        return carry

    lax.fori_loop(0, 8, score_step, 0)
    exchange_b(0)
    lax.fori_loop(8, 16, score_step, 0)
    exchange_c(0)

    w_load(3).wait()

    def gn_own(half, carry):
        gn[rows_of(hi * 2 + half, 256), :] = dot_nt(
            d[rows_of(half, 256), :], w[rows_of(hi, 512), :]
        ).astype(BF16)
        return carry

    lax.fori_loop(0, 2, gn_own, 0)
    exchange_end(0)

    def nm_copy(j, r):
        target = lax.rem(hi + offset(j), 4)
        return pltpu.make_async_remote_copy(
            src_ref=nm.at[rows_of(target * 4 + r, BLOCK), :],
            dst_ref=nr.at[rows_of(r, BLOCK), rows_of(hi, 512)],
            send_sem=nm_ssem.at[j, r],
            recv_sem=nm_rsem.at[j, r],
            device_id=across(offset(j)),
            device_id_type=MESH,
        )

    def nm_arrival(j, r):
        source = lax.rem(hi - offset(j) + 4, 4)
        return pltpu.make_async_remote_copy(
            src_ref=nm.at[rows_of(source * 4 + r, BLOCK), :],
            dst_ref=nr.at[rows_of(r, BLOCK), rows_of(source, 512)],
            send_sem=nm_ssem.at[j, r],
            recv_sem=nm_rsem.at[j, r],
            device_id=across(offset(j)),
            device_id_type=MESH,
        )

    def forward_step(i, carry):
        own = i // 12
        j = lax.rem(i, 3)
        r = (1 - own) * (i // 3) + own * (i - 12)
        b = lax.rem(hi + (1 - own) * offset(j), 4) * 4 + r
        rows = rows_of(b, BLOCK)
        for h in range(heads):
            cols = slice(h * HDIM, (h + 1) * HDIM)
            before = (rc[0, h * HDIM:(h + 1) * HDIM, :].astype(F32) + st[b, h]).astype(BF16)
            pb[b, h] = before
            attended = dot_nn(
                jnp.concatenate([sc[b, h], q[rows, cols]], axis=1),
                jnp.concatenate([v[rows, cols], before], axis=0),
            )
            inverse = lax.rsqrt(
                jnp.mean(attended * attended, axis=-1, keepdims=True) + EPSILON
            )
            scaled = attended * inverse
            unit[rows, cols] = scaled
            inv[rows, cols] = jnp.broadcast_to(inverse, (BLOCK, HDIM))
            nm[rows, cols] = (scaled * gain[:, cols].astype(F32)).astype(BF16)

        @pl.when(own == 0)
        def _():
            nm_copy(j, r).start()

        @pl.when(own == 1)
        def _():
            nr[rows_of(r, BLOCK), rows_of(hi, 512)] = nm[rows, :]

        return carry

    lax.fori_loop(0, nblocks, forward_step, 0)

    def gq_copy(b):
        rows = rows_of(b, BLOCK)
        return pltpu.make_async_copy(sq.at[rows, :], grad_query.at[rows, :], gq_sem.at[b])

    def gk_copy(b):
        rows = rows_of(b, BLOCK)
        return pltpu.make_async_copy(sk.at[rows, :], grad_key.at[rows, :], gk_sem.at[b])

    def gv_copy(b):
        rows = rows_of(b, BLOCK)
        return pltpu.make_async_copy(sv.at[rows, :], grad_value.at[rows, :], gv_sem.at[b])

    def backward_block(b):
        rows = rows_of(b, BLOCK)
        for h in range(heads):
            cols = slice(h * HDIM, (h + 1) * HDIM)
            grad_unit = gn[rows, cols].astype(F32) * gain[:, cols].astype(F32)
            scaled = unit[rows, cols]
            inner = jnp.mean(grad_unit * scaled, axis=-1, keepdims=True)
            grad = (inv[rows, cols] * (grad_unit - scaled * inner)).astype(BF16)
            g[rows, cols] = grad
            both = dot_nt(grad, jnp.concatenate([v[rows, cols], pb[b, h]], axis=0))
            weights = causal(both[:, :BLOCK])
            gsc[b, h] = weights
            bg[b, h] = dot_tn(q[rows, cols], grad)
            sq[rows, cols] = (dot_nn(weights, k[rows, cols]) + both[:, BLOCK:]).astype(BF16)
        gq_copy(b).start()

    def backward_step(i, carry):
        far_away = (i + 12) // 16
        t = jnp.maximum(i - 4, 0)
        j = lax.rem(t, 3)
        r = far_away * (t // 3) + (1 - far_away) * i

        @pl.when((far_away == 1) & (lax.rem(r, 2) == 0))
        def _():
            gn_arrival(j, r // 2).wait_recv()

        backward_block(lax.rem(hi - far_away * offset(j) + 4, 4) * 4 + r)
        return carry

    lax.fori_loop(0, nblocks, backward_step, 0)

    def suffix_step(i, total):
        b = nblocks - 1 - i
        fresh = bg[b]
        bg[b] = total
        return total + fresh

    def suffix_head(h):
        def step(i, total):
            b = nblocks - 1 - i
            fresh = bg[b, h]
            bg[b, h] = total
            return total + fresh

        return lax.fori_loop(0, nblocks, step, jnp.zeros((HDIM, HDIM), F32))

    for h in range(heads):
        st[0, h] = suffix_head(h)
    exchange_a(1, st[0])
    exchange_b(1)
    exchange_c(1)
    exchange_end(1)

    def final_step(b, carry):
        rows = rows_of(b, BLOCK)
        for h in range(heads):
            cols = slice(h * HDIM, (h + 1) * HDIM)
            after = (rc[1, h * HDIM:(h + 1) * HDIM, :].astype(F32) + bg[b, h]).astype(BF16)
            sk[rows, cols] = (
                dot_tn(gsc[b, h], q[rows, cols]) + dot_nt(v[rows, cols], after)
            ).astype(BF16)
            sv[rows, cols] = (
                dot_tn(sc[b, h], g[rows, cols]) + dot_nn(k[rows, cols], after)
            ).astype(BF16)
        gk_copy(b).start()
        gv_copy(b).start()
        return carry

    lax.fori_loop(0, nblocks, final_step, 0)

    def out_copy(r):
        rows = rows_of(r, BLOCK)
        return pltpu.make_async_copy(so.at[rows, :], out.at[rows, :], out_sem.at[r])

    def out_step(r, carry):
        for j in range(3):
            nm_arrival(j, r).wait_recv()
        rows = rows_of(r, BLOCK)

        def out_columns(n, inner):
            so[rows, rows_of(n, 512)] = dot_nn(nr[rows, :], w[:, rows_of(n, 512)]).astype(BF16)
            return inner

        lax.fori_loop(0, 4, out_columns, 0)
        out_copy(r).start()
        return carry

    lax.fori_loop(0, 4, out_step, 0)

    def drain(i, carry):
        j, r = i // 4, lax.rem(i, 4)
        nm_copy(j, r).wait_send()

        @pl.when(r < 2)
        def _():
            gn_copy(j, r).wait_send()

        return carry

    lax.fori_loop(0, 12, drain, 0)

    def drain_blocks(b, carry):
        gq_copy(b).wait()
        gk_copy(b).wait()
        gv_copy(b).wait()
        return carry

    lax.fori_loop(0, nblocks, drain_blocks, 0)
    for r in range(4):
        out_copy(r).wait()


def on_device(query, key, value, gain, w_out, d_out):
    tokens, width = query.shape
    hbm = pl.BlockSpec(memory_space=pl.ANY)
    vmem = pl.BlockSpec(memory_space=pltpu.VMEM)
    heads, nblocks = 4, 16
    tall = (tokens, width)
    squares = (nblocks, heads, HDIM, HDIM)
    dma = pltpu.SemaphoreType.DMA
    return pl.pallas_call(
        kernel,
        out_shape=(
            jax.ShapeDtypeStruct(d_out.shape, BF16),
            jax.ShapeDtypeStruct(tall, BF16),
            jax.ShapeDtypeStruct(tall, BF16),
            jax.ShapeDtypeStruct(tall, BF16),
        ),
        in_specs=[hbm, hbm, hbm, vmem, hbm, hbm],
        out_specs=(hbm, hbm, hbm, hbm),
        scratch_shapes=[
            pltpu.VMEM(tall, BF16),
            pltpu.VMEM(tall, BF16),
            pltpu.VMEM(tall, BF16),
            pltpu.VMEM(w_out.shape, BF16),
            pltpu.VMEM(d_out.shape, BF16),
            pltpu.VMEM((3, 512, width), BF16),
            pltpu.VMEM(tall, BF16),
            pltpu.VMEM(tall, BF16),
            pltpu.VMEM(d_out.shape, BF16),
            pltpu.VMEM(squares, BF16),
            pltpu.VMEM(squares, BF16),
            pltpu.VMEM(tall, BF16),
            pltpu.VMEM(squares, BF16),
            pltpu.VMEM((nblocks + 1, heads, HDIM, HDIM), F32),
            pltpu.VMEM(squares, F32),
            pltpu.VMEM(tall, F32),
            pltpu.VMEM(tall, F32),
            pltpu.VMEM(tall, BF16),
            pltpu.VMEM(tall, BF16),
            pltpu.VMEM(tall, BF16),
            pltpu.VMEM(d_out.shape, BF16),
            pltpu.VMEM((2, 512, HDIM), BF16),
            pltpu.VMEM((2, 8, 64, HDIM), BF16),
            pltpu.VMEM((2, 8, 64, HDIM), F32),
            pltpu.VMEM((2, 64, HDIM), F32),
            pltpu.VMEM((2, 4, 64, HDIM), F32),
            pltpu.VMEM((2, 8, 64, HDIM), BF16),
            pltpu.VMEM((2, 512, HDIM), BF16),
            dma((4,)), dma((4,)), dma((3, 2)), dma((3, 2)), dma((3, 4)), dma((3, 4)),
            dma((2, 7)), dma((2, 7)), dma((2, 3)), dma((2, 3)), dma((2, 7)), dma((2, 7)),
            dma((16,)), dma((16,)), dma((16,)), dma((4,)),
        ],
        compiler_params=pltpu.CompilerParams(
            collective_id=0, has_side_effects=True, vmem_limit_bytes=62 * 2**20
        ),
    )(query, key, value, gain.reshape(1, width), w_out, d_out)


def solution(mesh):
    in_specs = (
        P("ctx", "head"), P("ctx", "head"), P("ctx", "head"), P("head"), P(),
        P(("ctx", "head"), None),
    )
    out_specs = (
        P(("ctx", "head"), None), P("ctx", "head"), P("ctx", "head"), P("ctx", "head"),
    )
    return jax.shard_map(
        on_device, mesh=mesh, in_specs=in_specs, out_specs=out_specs, check_vma=False
    )
```

time: 216 us -> 80.6 us (0.37); the launches traced: 212 us -> 80.4 us
  Pallas kernels: 0 us -> 69.2 us
  local copies, waits for them, and re-layouts: 74.6 us -> 10.6 us
  blocking collectives: 54.4 us -> 0 us
  matrix products: 38 us -> 0 us
  other arithmetic: 21.5 us -> 0 us
  between operations: 14.4 us -> 0.65 us
  waiting for transfers between devices: 8.91 us -> 0 us
    pallas_call x0 -> x1, Pallas kernels: none -> 69.2 us  [on_device(): pl.pallas_call(kernel, out_shape=(jax.ShapeDtypeStruct(d_out.shape, BF16)...]
    all_gather x6 -> x0, blocking collectives: 54.4 us -> none  [prefix_by_axis(): pieces = lax.all_gather(total.astype(jnp.bfloat16), axis)]
    dot_general x14 -> x0, matrix products: 38 us -> none  [the longest x1 8.42 us: on_device(): jnp.dot(normed, w_slice, preferred_element_type=jnp.float32)]
    reshape x5 -> x1, local copies, waits for them, and re-layouts: 21.2 us -> 1.26 us  [on_device(): gain.reshape(1, width)]
    unnamed x44 -> x10, local copies, waits for them, and re-layouts: 25.4 us -> 9.32 us
    add x2 -> x0, local copies, waits for them, and re-layouts: 10.3 us -> none  [on_device(): attended + jnp.einsum('cshe,chef->cshf', q_blocks, prefixes, preferred_el...]
    rev x2 -> x0, local copies, waits for them, and re-layouts: 10.3 us -> none  [on_device(): tail_sums = jnp.cumsum(block_grads[::-1], axis=0)[::-1]]
    another operation x2 -> x0, other arithmetic: 9.16 us -> none  [the longest x1 6.42 us: on_device(): running = jnp.cumsum(block_states, axis=0)]
  transfers between devices with their start and end apart: 2 -> 0, of which waited for: 1 -> 0; matrix products, arithmetic and copies ran while one was open for 59% -> 0% of each run, Pallas kernels for 0% -> 0%
where the time goes in v1:
time: 80.6 us; the launch traced here: 80.4 us
  Pallas kernels  69.2 us (86%)
  local copies, waits for them, and re-layouts  10.6 us (13%)
    pallas_call x1, Pallas kernels, on_device(): pl.pallas_call(kernel, out_shape=(jax.ShapeDtypeStruct(d_out.shape, BF16)...  69.2 us
    unnamed x10, local copies, waits for them, and re-layouts  9.32 us

profile of v1, /device:TPU:1, one launch (start us, length us, event | category | flops | bytes accessed | tf_op | source)
XLA Modules:
  0.0 80.4 jit_solution(7377192972670828728)
XLA Ops:
  0.6 1.3 %reshape.11.gain = bf16[1,512]{1,0:T(2,128)(2,1)} reshape(bf16[512]{0:T(512)(128)(2,1)} %param.9) | data formatting | bytes 2048 | tf_op jit(solution)/shard_map/reshape | solution.py:469
  1.9 69.2 %shard_map.93 = (bf16[512,2048]{1,0:T(8,128)(2,1)}, bf16[2048,512]{1,0:T(8,128)(2,1)}, bf16[2048,512]{1,0:T(8,128)(2,1)}, bf16[2048,512]{1,0:T(8,128)(2,1)}) custom-call(bf16[2048,512]{1,0:T(8,128)(2,1)} %query.1, bf16[2048,512]{1,0:T(8,128)(2,1)} %key.1, bf16[2048,512]{1,0:T(8,128)(2,1)} %value.1, bf16[1,512]{1,0:T(2,128)(2,1)} %reshape.11.gain, ...), custom_call_target="tpu_custom_call" | custom-call | tf_op jit(solution)/shard_map/pallas_call | solution.py:423
  71.1 0.0 copy-start.2
  71.1 3.3 %copy.14 = bf16[512,2048]{1,0:T(8,128)(2,1)} copy(bf16[512,2048]{1,0:T(8,128)(2,1)} %get-tuple-element.8) | data formatting | bytes 4194304
  74.4 0.0 copy-done.2
  74.4 0.0 copy-start.1
  74.4 1.3 %copy.15 = bf16[2048,512]{1,0:T(8,128)(2,1)} copy(bf16[2048,512]{1,0:T(8,128)(2,1)S(1)} %copy-done.2) | data formatting | bytes 4194304
  75.7 1.0 %copy-done.1 = bf16[2048,512]{1,0:T(8,128)(2,1)S(1)} copy-done((bf16[2048,512]{1,0:T(8,128)(2,1)S(1)}, bf16[2048,512]{1,0:T(8,128)(2,1)}, u32[]{:S(2)}) %copy-start.1) | copy-done | bytes 2097176
  76.7 0.0 copy-start
  76.7 1.3 %copy.16 = bf16[2048,512]{1,0:T(8,128)(2,1)} copy(bf16[2048,512]{1,0:T(8,128)(2,1)S(1)} %copy-done.1) | data formatting | bytes 4194304
  78.1 1.0 %copy-done = bf16[2048,512]{1,0:T(8,128)(2,1)S(1)} copy-done((bf16[2048,512]{1,0:T(8,128)(2,1)S(1)}, bf16[2048,512]{1,0:T(8,128)(2,1)}, u32[]{:S(2)}) %copy-start) | copy-done | bytes 2097176
  79.1 1.3 %copy.17 = bf16[2048,512]{1,0:T(8,128)(2,1)} copy(bf16[2048,512]{1,0:T(8,128)(2,1)S(1)} %copy-done) | data formatting | bytes 4194304
Async XLA Ops:
  71.1 3.3 %copy-start.2 = (bf16[2048,512]{1,0:T(8,128)(2,1)S(1)}, bf16[2048,512]{1,0:T(8,128)(2,1)}, u32[]{:S(2)}) copy-start(bf16[2048,512]{1,0:T(8,128)(2,1)} %get-tuple-element.9) | copy-start | bytes 6291460
  74.4 2.3 %copy-start.1 = (bf16[2048,512]{1,0:T(8,128)(2,1)S(1)}, bf16[2048,512]{1,0:T(8,128)(2,1)}, u32[]{:S(2)}) copy-start(bf16[2048,512]{1,0:T(8,128)(2,1)} %get-tuple-element.10) | copy-start | bytes 6291460
  76.7 2.3 %copy-start = (bf16[2048,512]{1,0:T(8,128)(2,1)S(1)}, bf16[2048,512]{1,0:T(8,128)(2,1)}, u32[]{:S(2)}) copy-start(bf16[2048,512]{1,0:T(8,128)(2,1)} %get-tuple-element.11) | copy-start | bytes 6291460

commit v2 on v1

--- a/solution.py
+++ b/solution.py
@@ -31,11 +31,11 @@
 
 def kernel(
     query, key, value, gain, w_out, d_out,
-    out, grad_query, grad_key, grad_value,
-    q, k, v, w, d, gn_send, gn, nm, nr, sc, gsc, g, pb, st, bg, unit, inv, sq, sk, sv, so,
+    so, sq, sk, sv,
+    q, k, v, w, d, gn_send, gn, nm, nr, sc, gsc, g, pb, st, bg, unit, inv, run, acc,
     tb, ra, ea, rs, rb, pc, rc,
     load_sem, w_sem, gn_ssem, gn_rsem, nm_ssem, nm_rsem,
-    a_ssem, a_rsem, b_ssem, b_rsem, c_ssem, c_rsem, gq_sem, gk_sem, gv_sem, out_sem,
+    a_ssem, a_rsem, b_ssem, b_rsem, c_ssem, c_rsem,
 ):
     ci = lax.axis_index("ctx")
     hi = lax.axis_index("head")
@@ -44,23 +44,26 @@
     heads = 4
     nblocks = 16
 
-    pltpu.make_async_copy(d_out, d, load_sem.at[0]).start()
-
     def w_load(i):
         h = lax.rem(hi + (1 + 2 * i - 3 * (i // 2)) * (1 - i // 3), 4)
         return pltpu.make_async_copy(
             w_out.at[rows_of(h, 512), :], w.at[rows_of(h, 512), :], w_sem.at[i]
         )
 
-    for i in range(4):
-        w_load(i).start()
     loads = (
         pltpu.make_async_copy(key, k, load_sem.at[1]),
         pltpu.make_async_copy(value, v, load_sem.at[2]),
         pltpu.make_async_copy(query, q, load_sem.at[3]),
     )
-    for load in loads:
-        load.start()
+    pltpu.make_async_copy(d_out, d, load_sem.at[0]).start()
+    w_load(0).start()
+    w_load(1).start()
+    loads[0].start()
+    loads[1].start()
+    w_load(2).start()
+    loads[2].start()
+    w_load(3).start()
+    scales = gain[...].astype(F32).reshape(1, 512)
 
     def near(i):
         return {"ctx": y * 8 + lax.rem(me + i, 8)}
@@ -120,20 +123,25 @@
         gn_copy(j, half).start()
         return carry
 
-    lax.fori_loop(0, 6, gn_step, 0)
+    lax.fori_loop(0, 3, gn_step, 0)
 
     loads[0].wait()
     loads[1].wait()
-    st[0] = jnp.zeros((heads, HDIM, HDIM), F32)
-
-    def state_step(b, carry):
-        rows = rows_of(b, BLOCK)
+    run[...] = jnp.zeros((2, heads, HDIM, HDIM), F32)
+
+    def state_step(i, carry):
         for h in range(heads):
             cols = slice(h * HDIM, (h + 1) * HDIM)
-            st[b + 1, h] = st[b, h] + dot_tn(k[rows, cols], v[rows, cols])
-        return carry
-
-    lax.fori_loop(0, nblocks, state_step, 0)
+            total = run[0, h]
+            for u in range(4):
+                b = i * 4 + u
+                rows = rows_of(b, BLOCK)
+                st[b, h] = total
+                total = total + dot_tn(k[rows, cols], v[rows, cols])
+            run[0, h] = total
+        return carry
+
+    lax.fori_loop(0, 4, state_step, 0)
 
     def a_copy(way, i, slot):
         return pltpu.make_async_remote_copy(
@@ -200,8 +208,9 @@
         for i in range(1, 8):
             c_copy(way, i, lax.rem(me - i + 8, 8)).wait()
 
-    exchange_a(0, st[nblocks])
-
+    exchange_a(0, run[0])
+    lax.fori_loop(3, 6, gn_step, 0)
+    exchange_b(0)
     loads[2].wait()
 
     def causal(scores):
@@ -209,16 +218,16 @@
         col = lax.broadcasted_iota(jnp.int32, (BLOCK, BLOCK), 1)
         return jnp.where(col <= row, scores, jnp.zeros_like(scores)).astype(BF16)
 
-    def score_step(b, carry):
-        rows = rows_of(b, BLOCK)
-        for h in range(heads):
-            cols = slice(h * HDIM, (h + 1) * HDIM)
-            sc[b, h] = causal(dot_nt(q[rows, cols], k[rows, cols]))
-        return carry
-
-    lax.fori_loop(0, 8, score_step, 0)
-    exchange_b(0)
-    lax.fori_loop(8, 16, score_step, 0)
+    def score_step(i, carry):
+        for u in range(4):
+            b = i * 4 + u
+            rows = rows_of(b, BLOCK)
+            for h in range(heads):
+                cols = slice(h * HDIM, (h + 1) * HDIM)
+                sc[b, h] = causal(dot_nt(q[rows, cols], k[rows, cols]))
+        return carry
+
+    lax.fori_loop(0, 4, score_step, 0)
     exchange_c(0)
 
     w_load(3).wait()
@@ -232,33 +241,29 @@
     lax.fori_loop(0, 2, gn_own, 0)
     exchange_end(0)
 
-    def nm_copy(j, r):
+    def nm_copy(j, half):
         target = lax.rem(hi + offset(j), 4)
         return pltpu.make_async_remote_copy(
-            src_ref=nm.at[rows_of(target * 4 + r, BLOCK), :],
-            dst_ref=nr.at[rows_of(r, BLOCK), rows_of(hi, 512)],
-            send_sem=nm_ssem.at[j, r],
-            recv_sem=nm_rsem.at[j, r],
+            src_ref=nm.at[rows_of(target * 2 + half, 256), :],
+            dst_ref=nr.at[rows_of(half, 256), rows_of(hi, 512)],
+            send_sem=nm_ssem.at[j, half],
+            recv_sem=nm_rsem.at[j, half],
             device_id=across(offset(j)),
             device_id_type=MESH,
         )
 
-    def nm_arrival(j, r):
+    def nm_arrival(j, half):
         source = lax.rem(hi - offset(j) + 4, 4)
         return pltpu.make_async_remote_copy(
-            src_ref=nm.at[rows_of(source * 4 + r, BLOCK), :],
-            dst_ref=nr.at[rows_of(r, BLOCK), rows_of(source, 512)],
-            send_sem=nm_ssem.at[j, r],
-            recv_sem=nm_rsem.at[j, r],
+            src_ref=nm.at[rows_of(source * 2 + half, 256), :],
+            dst_ref=nr.at[rows_of(half, 256), rows_of(source, 512)],
+            send_sem=nm_ssem.at[j, half],
+            recv_sem=nm_rsem.at[j, half],
             device_id=across(offset(j)),
             device_id_type=MESH,
         )
 
-    def forward_step(i, carry):
-        own = i // 12
-        j = lax.rem(i, 3)
-        r = (1 - own) * (i // 3) + own * (i - 12)
-        b = lax.rem(hi + (1 - own) * offset(j), 4) * 4 + r
+    def forward_block(b):
         rows = rows_of(b, BLOCK)
         for h in range(heads):
             cols = slice(h * HDIM, (h + 1) * HDIM)
@@ -274,37 +279,33 @@
             scaled = attended * inverse
             unit[rows, cols] = scaled
             inv[rows, cols] = jnp.broadcast_to(inverse, (BLOCK, HDIM))
-            nm[rows, cols] = (scaled * gain[:, cols].astype(F32)).astype(BF16)
+            nm[rows, cols] = (scaled * scales[:, cols]).astype(BF16)
+
+    def forward_step(i, carry):
+        own = i // 6
+        j = lax.rem(i, 3)
+        half = (1 - own) * (i // 3) + own * (i - 6)
+        pair = lax.rem(hi + (1 - own) * offset(j), 4) * 2 + half
+        for u in range(2):
+            forward_block(pair * 2 + u)
 
         @pl.when(own == 0)
         def _():
-            nm_copy(j, r).start()
+            nm_copy(j, half).start()
 
         @pl.when(own == 1)
         def _():
-            nr[rows_of(r, BLOCK), rows_of(hi, 512)] = nm[rows, :]
-
-        return carry
-
-    lax.fori_loop(0, nblocks, forward_step, 0)
-
-    def gq_copy(b):
-        rows = rows_of(b, BLOCK)
-        return pltpu.make_async_copy(sq.at[rows, :], grad_query.at[rows, :], gq_sem.at[b])
-
-    def gk_copy(b):
-        rows = rows_of(b, BLOCK)
-        return pltpu.make_async_copy(sk.at[rows, :], grad_key.at[rows, :], gk_sem.at[b])
-
-    def gv_copy(b):
-        rows = rows_of(b, BLOCK)
-        return pltpu.make_async_copy(sv.at[rows, :], grad_value.at[rows, :], gv_sem.at[b])
+            nr[rows_of(half, 256), rows_of(hi, 512)] = nm[rows_of(pair, 256), :]
+
+        return carry
+
+    lax.fori_loop(0, 8, forward_step, 0)
 
     def backward_block(b):
         rows = rows_of(b, BLOCK)
         for h in range(heads):
             cols = slice(h * HDIM, (h + 1) * HDIM)
-            grad_unit = gn[rows, cols].astype(F32) * gain[:, cols].astype(F32)
+            grad_unit = gn[rows, cols].astype(F32) * scales[:, cols]
             scaled = unit[rows, cols]
             inner = jnp.mean(grad_unit * scaled, axis=-1, keepdims=True)
             grad = (inv[rows, cols] * (grad_unit - scaled * inner)).astype(BF16)
@@ -312,30 +313,28 @@
             both = dot_nt(grad, jnp.concatenate([v[rows, cols], pb[b, h]], axis=0))
             weights = causal(both[:, :BLOCK])
             gsc[b, h] = weights
-            bg[b, h] = dot_tn(q[rows, cols], grad)
+            fresh = dot_tn(q[rows, cols], grad)
+            bg[b, h] = fresh
+            run[1, h] = run[1, h] + fresh
             sq[rows, cols] = (dot_nn(weights, k[rows, cols]) + both[:, BLOCK:]).astype(BF16)
-        gq_copy(b).start()
 
     def backward_step(i, carry):
-        far_away = (i + 12) // 16
-        t = jnp.maximum(i - 4, 0)
+        far_away = (i + 6) // 8
+        t = jnp.maximum(i - 2, 0)
         j = lax.rem(t, 3)
-        r = far_away * (t // 3) + (1 - far_away) * i
-
-        @pl.when((far_away == 1) & (lax.rem(r, 2) == 0))
+        half = far_away * (t // 3) + (1 - far_away) * i
+
+        @pl.when(far_away == 1)
         def _():
-            gn_arrival(j, r // 2).wait_recv()
-
-        backward_block(lax.rem(hi - far_away * offset(j) + 4, 4) * 4 + r)
-        return carry
-
-    lax.fori_loop(0, nblocks, backward_step, 0)
-
-    def suffix_step(i, total):
-        b = nblocks - 1 - i
-        fresh = bg[b]
-        bg[b] = total
-        return total + fresh
+            gn_arrival(j, half).wait_recv()
+
+        pair = lax.rem(hi - far_away * offset(j) + 4, 4) * 2 + half
+        for u in range(2):
+            backward_block(pair * 2 + u)
+        return carry
+
+    lax.fori_loop(0, 8, backward_step, 0)
+    exchange_a(1, run[1])
 
     def suffix_head(h):
         def step(i, total):
@@ -347,13 +346,21 @@
         return lax.fori_loop(0, nblocks, step, jnp.zeros((HDIM, HDIM), F32))
 
     for h in range(heads):
-        st[0, h] = suffix_head(h)
-    exchange_a(1, st[0])
+        suffix_head(h)
     exchange_b(1)
     exchange_c(1)
+
+    for j in range(3):
+        nm_arrival(j, 0).wait_recv()
+
+    def out_columns(n, carry):
+        so[:256, rows_of(n, 512)] = dot_nn(nr[:256, :], w[:, rows_of(n, 512)]).astype(BF16)
+        return carry
+
+    lax.fori_loop(0, 4, out_columns, 0)
     exchange_end(1)
 
-    def final_step(b, carry):
+    def final_block(b):
         rows = rows_of(b, BLOCK)
         for h in range(heads):
             cols = slice(h * HDIM, (h + 1) * HDIM)
@@ -364,52 +371,57 @@
             sv[rows, cols] = (
                 dot_tn(sc[b, h], g[rows, cols]) + dot_nn(k[rows, cols], after)
             ).astype(BF16)
-        gk_copy(b).start()
-        gv_copy(b).start()
-        return carry
-
-    lax.fori_loop(0, nblocks, final_step, 0)
-
-    def out_copy(r):
-        rows = rows_of(r, BLOCK)
-        return pltpu.make_async_copy(so.at[rows, :], out.at[rows, :], out_sem.at[r])
-
-    def out_step(r, carry):
-        for j in range(3):
-            nm_arrival(j, r).wait_recv()
-        rows = rows_of(r, BLOCK)
-
-        def out_columns(n, inner):
-            so[rows, rows_of(n, 512)] = dot_nn(nr[rows, :], w[:, rows_of(n, 512)]).astype(BF16)
-            return inner
-
-        lax.fori_loop(0, 4, out_columns, 0)
-        out_copy(r).start()
-        return carry
-
-    lax.fori_loop(0, 4, out_step, 0)
-
-    def drain(i, carry):
-        j, r = i // 4, lax.rem(i, 4)
-        nm_copy(j, r).wait_send()
-
-        @pl.when(r < 2)
-        def _():
-            gn_copy(j, r).wait_send()
-
-        return carry
-
-    lax.fori_loop(0, 12, drain, 0)
-
-    def drain_blocks(b, carry):
-        gq_copy(b).wait()
-        gk_copy(b).wait()
-        gv_copy(b).wait()
-        return carry
-
-    lax.fori_loop(0, nblocks, drain_blocks, 0)
-    for r in range(4):
-        out_copy(r).wait()
+
+    def final_step(i, carry):
+        for u in range(2):
+            final_block(i * 2 + u)
+        return carry
+
+    lax.fori_loop(0, 8, final_step, 0)
+
+    def late_part(source, n):
+        return dot_nn(
+            nr[256:, rows_of(source, 512)], w[rows_of(source, 512), rows_of(n, 512)]
+        )
+
+    def late_own(n, carry):
+        acc[:, rows_of(n, 512)] = late_part(hi, n)
+        return carry
+
+    lax.fori_loop(0, 4, late_own, 0)
+    for j in range(2):
+        nm_arrival(j, 1).wait_recv()
+
+        def late_add(n, carry):
+            source = lax.rem(hi - offset(j) + 4, 4)
+            cols = rows_of(n, 512)
+            acc[:, cols] = acc[:, cols] + late_part(source, n)
+            return carry
+
+        lax.fori_loop(0, 4, late_add, 0)
+    nm_arrival(2, 1).wait_recv()
+
+    def late_last(n, carry):
+        cols = rows_of(n, 512)
+        so[256:, cols] = (acc[:, cols] + late_part(lax.rem(hi + 2, 4), n)).astype(BF16)
+        return carry
+
+    lax.fori_loop(0, 4, late_last, 0)
+    for j in range(3):
+        for half in range(2):
+            gn_copy(j, half).wait_send()
+            nm_copy(j, half).wait_send()
+
+
+def store_kernel(a, b, c, d, a_out, b_out, c_out, d_out, sem):
+    copies = [
+        pltpu.make_async_copy(held, placed, sem.at[i])
+        for i, (held, placed) in enumerate(((a, a_out), (b, b_out), (c, c_out), (d, d_out)))
+    ]
+    for copy in copies:
+        copy.start()
+    for copy in copies:
+        copy.wait()
 
 
 def on_device(query, key, value, gain, w_out, d_out):
@@ -420,16 +432,16 @@
     tall = (tokens, width)
     squares = (nblocks, heads, HDIM, HDIM)
     dma = pltpu.SemaphoreType.DMA
-    return pl.pallas_call(
+    held = pl.pallas_call(
         kernel,
         out_shape=(
-            jax.ShapeDtypeStruct(d_out.shape, BF16),
-            jax.ShapeDtypeStruct(tall, BF16),
-            jax.ShapeDtypeStruct(tall, BF16),
-            jax.ShapeDtypeStruct(tall, BF16),
+            pltpu.VMEM(d_out.shape, BF16),
+            pltpu.VMEM(tall, BF16),
+            pltpu.VMEM(tall, BF16),
+            pltpu.VMEM(tall, BF16),
         ),
         in_specs=[hbm, hbm, hbm, vmem, hbm, hbm],
-        out_specs=(hbm, hbm, hbm, hbm),
+        out_specs=(vmem, vmem, vmem, vmem),
         scratch_shapes=[
             pltpu.VMEM(tall, BF16),
             pltpu.VMEM(tall, BF16),
@@ -444,14 +456,12 @@
             pltpu.VMEM(squares, BF16),
             pltpu.VMEM(tall, BF16),
             pltpu.VMEM(squares, BF16),
-            pltpu.VMEM((nblocks + 1, heads, HDIM, HDIM), F32),
+            pltpu.VMEM(squares, F32),
             pltpu.VMEM(squares, F32),
             pltpu.VMEM(tall, F32),
             pltpu.VMEM(tall, F32),
-            pltpu.VMEM(tall, BF16),
-            pltpu.VMEM(tall, BF16),
-            pltpu.VMEM(tall, BF16),
-            pltpu.VMEM(d_out.shape, BF16),
+            pltpu.VMEM((2, heads, HDIM, HDIM), F32),
+            pltpu.VMEM((256, d_out.shape[1]), F32),
             pltpu.VMEM((2, 512, HDIM), BF16),
             pltpu.VMEM((2, 8, 64, HDIM), BF16),
             pltpu.VMEM((2, 8, 64, HDIM), F32),
@@ -459,14 +469,21 @@
             pltpu.VMEM((2, 4, 64, HDIM), F32),
             pltpu.VMEM((2, 8, 64, HDIM), BF16),
             pltpu.VMEM((2, 512, HDIM), BF16),
-            dma((4,)), dma((4,)), dma((3, 2)), dma((3, 2)), dma((3, 4)), dma((3, 4)),
+            dma((4,)), dma((4,)), dma((3, 2)), dma((3, 2)), dma((3, 2)), dma((3, 2)),
             dma((2, 7)), dma((2, 7)), dma((2, 3)), dma((2, 3)), dma((2, 7)), dma((2, 7)),
-            dma((16,)), dma((16,)), dma((16,)), dma((4,)),
         ],
         compiler_params=pltpu.CompilerParams(
-            collective_id=0, has_side_effects=True, vmem_limit_bytes=62 * 2**20
+            collective_id=0, has_side_effects=True, vmem_limit_bytes=54 * 2**20
         ),
-    )(query, key, value, gain.reshape(1, width), w_out, d_out)
+    )(query, key, value, gain, w_out, d_out)
+    return pl.pallas_call(
+        store_kernel,
+        out_shape=tuple(jax.ShapeDtypeStruct(x.shape, BF16) for x in held),
+        in_specs=[vmem] * 4,
+        out_specs=(hbm,) * 4,
+        scratch_shapes=[dma((4,))],
+        compiler_params=pltpu.CompilerParams(vmem_limit_bytes=2**20),
+    )(*held)
 
 
 def solution(mesh):

time: 80.6 us -> 63.5 us (0.79)
  local copies, waits for them, and re-layouts: 10.6 us -> 0 us
  Pallas kernels: 69.2 us -> 62.8 us
    unnamed x10 -> x0, local copies, waits for them, and re-layouts: 9.32 us -> none
    pallas_call x1 -> x2, Pallas kernels: 69.2 us -> 62.8 us  [the longest x1 59.4 us: on_device(): pl.pallas_call(kernel, out_shape=(pltpu.VMEM(d_out.shape, BF16), pltpu.VM...]
    reshape x1 -> x0, local copies, waits for them, and re-layouts: 1.26 us -> none  [on_device(): gain.reshape(1, width)]
where the time goes in v2:
time: 63.5 us; the launch traced here: 63.4 us
  Pallas kernels  62.8 us (99%)
  between operations  0.64 us (1%)
    pallas_call x1, Pallas kernels, on_device(): pl.pallas_call(kernel, out_shape=(pltpu.VMEM(d_out.shape, BF16), pltpu.VM...  59.4 us
    pallas_call x1, Pallas kernels, on_device(): pl.pallas_call(store_kernel, out_shape=tuple((jax.ShapeDtypeStruct(x.shap...  3.37 us

profile of v2, /device:TPU:1, one launch (start us, length us, event | category | flops | bytes accessed | tf_op | source)
XLA Modules:
  0.0 63.4 jit_solution(15686090733340467798)
XLA Ops:
  0.6 59.4 %shard_map.93 = (bf16[512,2048]{1,0:T(8,128)(2,1)S(1)}, bf16[2048,512]{1,0:T(8,128)(2,1)S(1)}, bf16[2048,512]{1,0:T(8,128)(2,1)S(1)}, bf16[2048,512]{1,0:T(8,128)(2,1)S(1)}) custom-call(bf16[2048,512]{1,0:T(8,128)(2,1)} %query.1, bf16[2048,512]{1,0:T(8,128)(2,1)} %key.1, bf16[2048,512]{1,0:T(8,128)(2,1)} %value.1, bf16[512]{0:T(512)(128)(2,1)} %gain.1, ...), custom_call_target="tpu_custom_call" | custom-call | tf_op jit(solution)/shard_map/pallas_call | solution.py:435
  60.0 3.4 %shard_map.94 = (bf16[512,2048]{1,0:T(8,128)(2,1)}, bf16[2048,512]{1,0:T(8,128)(2,1)}, bf16[2048,512]{1,0:T(8,128)(2,1)}, bf16[2048,512]{1,0:T(8,128)(2,1)}) custom-call(bf16[512,2048]{1,0:T(8,128)(2,1)S(1)} %get-tuple-element.8.a, bf16[2048,512]{1,0:T(8,128)(2,1)S(1)} %get-tuple-element.9.b, bf16[2048,512]{1,0:T(8,128)(2,1)S(1)} %get-tuple-element.10.c, ...), custom_call_target="tpu_custom_call" | custom-call | tf_op jit(solution)/shard_map/pallas_call | solution.py:479

commit v3 on v2

--- a/solution.py
+++ b/solution.py
@@ -31,8 +31,8 @@
 
 def kernel(
     query, key, value, gain, w_out, d_out,
-    so, sq, sk, sv,
-    q, k, v, w, d, gn_send, gn, nm, nr, sc, gsc, g, pb, st, bg, unit, inv, run, acc,
+    so, sq, sk, sv, acc, nl, wl,
+    q, k, v, w, d, gn_send, gn, nm, nr, sc, gsc, g, pb, st, bg, unit, inv, run,
     tb, ra, ea, rs, rb, pc, rc,
     load_sem, w_sem, gn_ssem, gn_rsem, nm_ssem, nm_rsem,
     a_ssem, a_rsem, b_ssem, b_rsem, c_ssem, c_rsem,
@@ -55,14 +55,17 @@
         pltpu.make_async_copy(value, v, load_sem.at[2]),
         pltpu.make_async_copy(query, q, load_sem.at[3]),
     )
-    pltpu.make_async_copy(d_out, d, load_sem.at[0]).start()
+    d_loads = [
+        pltpu.make_async_copy(
+            d_out.at[rows_of(half, 256), :], d.at[rows_of(half, 256), :], load_sem.at[4 * half]
+        )
+        for half in range(2)
+    ]
+    wl_load = pltpu.make_async_copy(
+        w_out.at[rows_of(lax.rem(hi + 2, 4), 512), :], wl, load_sem.at[5]
+    )
+    d_loads[0].start()
     w_load(0).start()
-    w_load(1).start()
-    loads[0].start()
-    loads[1].start()
-    w_load(2).start()
-    loads[2].start()
-    w_load(3).start()
     scales = gain[...].astype(F32).reshape(1, 512)
 
     def near(i):
@@ -107,7 +110,7 @@
             device_id_type=MESH,
         )
 
-    pltpu.make_async_copy(d_out, d, load_sem.at[0]).wait()
+    d_loads[0].wait()
 
     def gn_step(i, carry):
         half, j = i // 3, lax.rem(i, 3)
@@ -115,6 +118,16 @@
         @pl.when(half == 0)
         def _():
             w_load(j).wait()
+
+        @pl.when(i == 0)
+        def _():
+            w_load(1).start()
+            w_load(2).start()
+            for load in loads:
+                load.start()
+            d_loads[1].start()
+            w_load(3).start()
+            wl_load.start()
 
         h = lax.rem(hi + offset(j), 4)
         gn_send[j, rows_of(half, 256), :] = dot_nt(
@@ -186,8 +199,8 @@
         for s in reversed(range(8)) if way else range(8):
             ea[way, s] = run
             run = run + ra[way, s].astype(F32)
-        rs[way] = run
-        rb[way, y] = jnp.zeros((64, HDIM), F32)
+        rs[way] = run.astype(BF16)
+        rb[way, y] = jnp.zeros((64, HDIM), BF16)
         for i in range(1, 4):
             b_copy(way, i, y).start()
 
@@ -197,7 +210,7 @@
         base = jnp.zeros((64, HDIM), F32)
         for s in range(4):
             passed = s > y if way else s < y
-            base = base + jnp.where(passed, rb[way, s], jnp.zeros((64, HDIM), F32))
+            base = base + jnp.where(passed, rb[way, s].astype(F32), jnp.zeros((64, HDIM), F32))
         for s in range(8):
             pc[way, s] = (base + ea[way, s]).astype(BF16)
         rc[way, rows_of(me, 64), :] = pc[way, me]
@@ -209,6 +222,7 @@
             c_copy(way, i, lax.rem(me - i + 8, 8)).wait()
 
     exchange_a(0, run[0])
+    d_loads[1].wait()
     lax.fori_loop(3, 6, gn_step, 0)
     exchange_b(0)
     loads[2].wait()
@@ -354,7 +368,7 @@
         nm_arrival(j, 0).wait_recv()
 
     def out_columns(n, carry):
-        so[:256, rows_of(n, 512)] = dot_nn(nr[:256, :], w[:, rows_of(n, 512)]).astype(BF16)
+        so[:, rows_of(n, 512)] = dot_nn(nr[:256, :], w[:, rows_of(n, 512)]).astype(BF16)
         return carry
 
     lax.fori_loop(0, 4, out_columns, 0)
@@ -384,42 +398,43 @@
             nr[256:, rows_of(source, 512)], w[rows_of(source, 512), rows_of(n, 512)]
         )
 
-    def late_own(n, carry):
-        acc[:, rows_of(n, 512)] = late_part(hi, n)
-        return carry
-
-    lax.fori_loop(0, 4, late_own, 0)
     for j in range(2):
         nm_arrival(j, 1).wait_recv()
 
-        def late_add(n, carry):
-            source = lax.rem(hi - offset(j) + 4, 4)
-            cols = rows_of(n, 512)
-            acc[:, cols] = acc[:, cols] + late_part(source, n)
-            return carry
-
-        lax.fori_loop(0, 4, late_add, 0)
+    def late_most(n, carry):
+        total = late_part(hi, n)
+        for j in range(2):
+            total = total + late_part(lax.rem(hi - offset(j) + 4, 4), n)
+        acc[:, rows_of(n, 512)] = total
+        return carry
+
+    lax.fori_loop(0, 4, late_most, 0)
+    wl_load.wait()
     nm_arrival(2, 1).wait_recv()
-
-    def late_last(n, carry):
-        cols = rows_of(n, 512)
-        so[256:, cols] = (acc[:, cols] + late_part(lax.rem(hi + 2, 4), n)).astype(BF16)
-        return carry
-
-    lax.fori_loop(0, 4, late_last, 0)
+    nl[...] = nr[256:, rows_of(lax.rem(hi + 2, 4), 512)]
     for j in range(3):
         for half in range(2):
             gn_copy(j, half).wait_send()
             nm_copy(j, half).wait_send()
 
 
-def store_kernel(a, b, c, d, a_out, b_out, c_out, d_out, sem):
+def store_kernel(so, sq, sk, sv, acc, nl, wl, out, grad_query, grad_key, grad_value, late, sem):
     copies = [
         pltpu.make_async_copy(held, placed, sem.at[i])
-        for i, (held, placed) in enumerate(((a, a_out), (b, b_out), (c, c_out), (d, d_out)))
+        for i, (held, placed) in enumerate(
+            ((sq, grad_query), (sk, grad_key), (sv, grad_value), (so, out.at[pl.ds(0, 256), :]))
+        )
     ]
     for copy in copies:
         copy.start()
+    for n in range(4):
+        cols = pl.ds(n * 512, 512)
+        late[:, cols] = (acc[:, cols] + dot_nn(nl[...], wl[:, cols])).astype(BF16)
+        copy = pltpu.make_async_copy(
+            late.at[:, cols], out.at[pl.ds(256, 256), cols], sem.at[4 + n]
+        )
+        copy.start()
+        copies.append(copy)
     for copy in copies:
         copy.wait()
 
@@ -435,13 +450,16 @@
     held = pl.pallas_call(
         kernel,
         out_shape=(
-            pltpu.VMEM(d_out.shape, BF16),
-            pltpu.VMEM(tall, BF16),
-            pltpu.VMEM(tall, BF16),
-            pltpu.VMEM(tall, BF16),
+            pltpu.VMEM((256, d_out.shape[1]), BF16),
+            pltpu.VMEM(tall, BF16),
+            pltpu.VMEM(tall, BF16),
+            pltpu.VMEM(tall, BF16),
+            pltpu.VMEM((256, d_out.shape[1]), F32),
+            pltpu.VMEM((256, width), BF16),
+            pltpu.VMEM((width, d_out.shape[1]), BF16),
         ),
         in_specs=[hbm, hbm, hbm, vmem, hbm, hbm],
-        out_specs=(vmem, vmem, vmem, vmem),
+        out_specs=(vmem,) * 7,
         scratch_shapes=[
             pltpu.VMEM(tall, BF16),
             pltpu.VMEM(tall, BF16),
@@ -461,28 +479,29 @@
             pltpu.VMEM(tall, F32),
             pltpu.VMEM(tall, F32),
             pltpu.VMEM((2, heads, HDIM, HDIM), F32),
-            pltpu.VMEM((256, d_out.shape[1]), F32),
             pltpu.VMEM((2, 512, HDIM), BF16),
             pltpu.VMEM((2, 8, 64, HDIM), BF16),
             pltpu.VMEM((2, 8, 64, HDIM), F32),
-            pltpu.VMEM((2, 64, HDIM), F32),
-            pltpu.VMEM((2, 4, 64, HDIM), F32),
+            pltpu.VMEM((2, 64, HDIM), BF16),
+            pltpu.VMEM((2, 4, 64, HDIM), BF16),
             pltpu.VMEM((2, 8, 64, HDIM), BF16),
             pltpu.VMEM((2, 512, HDIM), BF16),
-            dma((4,)), dma((4,)), dma((3, 2)), dma((3, 2)), dma((3, 2)), dma((3, 2)),
+            dma((6,)), dma((4,)), dma((3, 2)), dma((3, 2)), dma((3, 2)), dma((3, 2)),
             dma((2, 7)), dma((2, 7)), dma((2, 3)), dma((2, 3)), dma((2, 7)), dma((2, 7)),
         ],
         compiler_params=pltpu.CompilerParams(
-            collective_id=0, has_side_effects=True, vmem_limit_bytes=54 * 2**20
+            collective_id=0, has_side_effects=True, vmem_limit_bytes=51 * 2**20
         ),
     )(query, key, value, gain, w_out, d_out)
     return pl.pallas_call(
         store_kernel,
-        out_shape=tuple(jax.ShapeDtypeStruct(x.shape, BF16) for x in held),
-        in_specs=[vmem] * 4,
+        out_shape=tuple(
+            jax.ShapeDtypeStruct(shape, BF16) for shape in (d_out.shape, tall, tall, tall)
+        ),
+        in_specs=[vmem] * 7,
         out_specs=(hbm,) * 4,
-        scratch_shapes=[dma((4,))],
-        compiler_params=pltpu.CompilerParams(vmem_limit_bytes=2**20),
+        scratch_shapes=[pltpu.VMEM((256, d_out.shape[1]), BF16), dma((8,))],
+        compiler_params=pltpu.CompilerParams(vmem_limit_bytes=4 * 2**20),
     )(*held)
 
 

time: 63.5 us -> 60.4 us (0.951)
  Pallas kernels: 62.8 us -> 59.4 us
    pallas_call x2, Pallas kernels: 62.8 us -> 59.4 us  [the longest x1 56.1 us: on_device(): pl.pallas_call(kernel, out_shape=(pltpu.VMEM((256, d_out.shape[1]), BF16)...]
where the time goes in v3:
time: 60.4 us; the launch traced here: 60.1 us
  Pallas kernels  59.4 us (98%)
  between operations  0.64 us (1%)
    pallas_call x1, Pallas kernels, on_device(): pl.pallas_call(kernel, out_shape=(pltpu.VMEM((256, d_out.shape[1]), BF16)...  56.1 us
    pallas_call x1, Pallas kernels, on_device(): pl.pallas_call(store_kernel, out_shape=tuple((jax.ShapeDtypeStruct(shape,...  3.34 us

profile of v3, /device:TPU:1, one launch (start us, length us, event | category | flops | bytes accessed | tf_op | source)
XLA Modules:
  0.0 60.1 jit_solution(3830557257343906520)
XLA Ops:
  0.6 56.1 %shard_map.93 = (bf16[256,2048]{1,0:T(8,128)(2,1)S(1)}, bf16[2048,512]{1,0:T(8,128)(2,1)S(1)}, bf16[2048,512]{1,0:T(8,128)(2,1)S(1)}, bf16[2048,512]{1,0:T(8,128...) custom-call(bf16[2048,512]{1,0:T(8,128)(2,1)} %query.1, ...), custom_call_target="tpu_custom_call" | custom-call | tf_op jit(solution)/shard_map/pallas_call | solution.py:450
  56.7 3.3 %shard_map.94 = (bf16[512,2048]{1,0:T(8,128)(2,1)}, bf16[2048,512]{1,0:T(8,128)(2,1)}, bf16[2048,512]{1,0:T(8,128)(2,1)}, bf16[2048,512]{1,0:T(8,128)(2,1)}) custom-call(bf16[256,2048]{1,0:T(8,128)(2,1)S(1)} %get-tuple-element.11.so, bf16[2048,512]{1,0:T(8,128)(2,1)S(1)} %get-tuple-element.12.sq, bf16[2048,512]{1,0:T(8,128)(2,1)S(1)} %get-tuple-element.13.sk, ...), custom_call_target="tpu_custom_call" | custom-call | tf_op jit(solution)/shard_map/pallas_call | solution.py:496

commit v4 on v3

--- a/solution.py
+++ b/solution.py
@@ -387,11 +387,11 @@
             ).astype(BF16)
 
     def final_step(i, carry):
-        for u in range(2):
-            final_block(i * 2 + u)
-        return carry
-
-    lax.fori_loop(0, 8, final_step, 0)
+        for u in range(4):
+            final_block(i * 4 + u)
+        return carry
+
+    lax.fori_loop(0, 4, final_step, 0)
 
     def late_part(source, n):
         return dot_nn(

time: 60.4 us -> 60.4 us (level)
  no operation moved by 1% of the time
where the time goes in v4:
time: 60.4 us; the launch traced here: 60.1 us
  Pallas kernels  59.4 us (98%)
  between operations  0.64 us (1%)
    pallas_call x1, Pallas kernels, on_device(): pl.pallas_call(kernel, out_shape=(pltpu.VMEM((256, d_out.shape[1]), BF16)...  56.1 us
    pallas_call x1, Pallas kernels, on_device(): pl.pallas_call(store_kernel, out_shape=tuple((jax.ShapeDtypeStruct(shape,...  3.34 us

profile of v4, /device:TPU:1, one launch (start us, length us, event | category | flops | bytes accessed | tf_op | source)
XLA Modules:
  0.0 60.1 jit_solution(778967127420308086)
XLA Ops:
  0.6 56.1 %shard_map.93 = (bf16[256,2048]{1,0:T(8,128)(2,1)S(1)}, bf16[2048,512]{1,0:T(8,128)(2,1)S(1)}, bf16[2048,512]{1,0:T(8,128)(2,1)S(1)}, bf16[2048,512]{1,0:T(8,128...) custom-call(bf16[2048,512]{1,0:T(8,128)(2,1)} %query.1, ...), custom_call_target="tpu_custom_call" | custom-call | tf_op jit(solution)/shard_map/pallas_call | solution.py:450
  56.7 3.3 %shard_map.94 = (bf16[512,2048]{1,0:T(8,128)(2,1)}, bf16[2048,512]{1,0:T(8,128)(2,1)}, bf16[2048,512]{1,0:T(8,128)(2,1)}, bf16[2048,512]{1,0:T(8,128)(2,1)}) custom-call(bf16[256,2048]{1,0:T(8,128)(2,1)S(1)} %get-tuple-element.11.so, bf16[2048,512]{1,0:T(8,128)(2,1)S(1)} %get-tuple-element.12.sq, bf16[2048,512]{1,0:T(8,128)(2,1)S(1)} %get-tuple-element.13.sk, ...), custom_call_target="tpu_custom_call" | custom-call | tf_op jit(solution)/shard_map/pallas_call | solution.py:496
